TPU v7x, 32 devices: a whole 2x2x4 slice. The times are simulated.
32 devices in a mesh: gx: 4 (over y, core), gy: 4 (over z), gz: 2 (over x).
Axes of the slice: x: 2, y: 2, z: 4, core: 2. Of those that a mesh axis runs over, the one named last changes fastest.
Arguments:
- residual: float32 [32, 128, 256], P('gx', 'gy', 'gz'), may hold values from -32 to 32
- direction: float32 [32, 128, 256], P('gx', 'gy', 'gz'), may hold values from -32 to 32
- diagonal: float32 [32, 128, 256], P('gx', 'gy', 'gz'), may hold values from 0.5 to 2
- recycled: bfloat16 [16, 32, 128, 256], P(None, 'gx', 'gy', 'gz'), may hold values from -6 to 6
- recycled_images: bfloat16 [16, 32, 128, 256], P(None, 'gx', 'gy', 'gz'), may hold values from -0.0014648438 to 0.0014648438
- coupling_inverse: float32 [16, 16], replicated, may hold values from -1 to 3, as said below
Outputs:
- solution_delta: float32 [32, 128, 256], P('gx', 'gy', 'gz')
- new_residual: float32 [32, 128, 256], P('gx', 'gy', 'gz')
- new_direction: float32 [32, 128, 256], P('gx', 'gy', 'gz')
Inputs may be any that keep to these rules, and one draw needn't show every extreme that they name: `coupling_inverse`: symmetric.
All inputs are finite; a program needn't handle non-finite values.
Results may differ from a plain program's by a relative error of at most 0.0028.
Values sent between devices are 32-bit elements; how exact they have to be, the bound alone decides.
No kernel may reach another device: no remote copies, remote signals or barrier semaphores. Data moves between devices by JAX's collectives and lax.ppermute only.
A program may use at most 64 MiB of HBM per device.

v0:
```python
import jax
import jax.numpy as jnp
import numpy as np
from jax import lax
from jax.sharding import PartitionSpec as P

S = 4
BASIS = 9


center = 7.25
half_width = 6.75


def extended(block, sides, width):
    for axis, dim in sides:
        count = lax.axis_size(axis)
        forward = [(i, i + 1) for i in range(count - 1)]
        forward.append((count - 1, 0))
        backward = [(target, source) for source, target in forward]
        low = lax.ppermute(
            lax.slice_in_dim(block, block.shape[dim] - width, None, axis=dim), axis, forward
        )
        high = lax.ppermute(lax.slice_in_dim(block, 0, width, axis=dim), axis, backward)
        block = jnp.concatenate([low, block, high], axis=dim)
    return block


def inside(padded):
    centre_cells = padded[:, 1:-1, 1:-1, 1:-1]
    beside_all = padded[:, 2:, 1:-1, 1:-1] + padded[:, :-2, 1:-1, 1:-1]
    beside_all = beside_all + padded[:, 1:-1, 2:, 1:-1] + padded[:, 1:-1, :-2, 1:-1]
    beside_all = beside_all + padded[:, 1:-1, 1:-1, 2:] + padded[:, 1:-1, 1:-1, :-2]
    return (centre_cells, beside_all)


def trim_margin(values, margin):
    if margin == 0:
        return values
    return values[..., margin:-margin, margin:-margin, margin:-margin]


def chebyshev_next(current, beside_all, diagonal, earlier):
    mapped = (6.0 + diagonal) * current - beside_all
    scaled = (mapped - center * current) / half_width
    if earlier is None:
        return scaled
    return 2.0 * scaled - earlier


def recurrence_matrix():
    recurrence = np.zeros((BASIS, BASIS), np.float32)
    for offset, length in ((0, S + 1), (S + 1, S)):
        recurrence[offset, offset] = center
        recurrence[offset + 1, offset] = half_width
        for column in range(1, length - 1):
            recurrence[offset + column + 1, offset + column] = half_width / 2
            recurrence[offset + column, offset + column] = center
            recurrence[offset + column - 1, offset + column] = half_width / 2
    return jnp.asarray(recurrence, dtype=jnp.float32)


def coordinates(totals, coupling_inverse):
    precise = lax.Precision.HIGHEST
    gram_block = totals[:BASIS]
    projections = totals[BASIS:]
    recurrence = recurrence_matrix()
    counter = jnp.arange(BASIS)
    residue = (counter == S + 1).astype(jnp.float32)
    search = (counter == 0).astype(jnp.float32)
    update = jnp.zeros((BASIS,), jnp.float32)
    norm_now = jnp.dot(residue, jnp.dot(gram_block, residue, precision=precise), precision=precise)
    for iteration in range(S):
        mapped = jnp.dot(recurrence, search, precision=precise)
        step_size = norm_now / jnp.dot(
            search, jnp.dot(gram_block, mapped, precision=precise), precision=precise
        )
        update = update + step_size * search
        residue = residue - step_size * mapped
        norm_next = jnp.dot(
            residue, jnp.dot(gram_block, residue, precision=precise), precision=precise
        )
        search = residue + norm_next / norm_now * search
        norm_now = norm_next
    weights = jnp.dot(
        coupling_inverse, jnp.dot(projections, residue, precision=precise), precision=precise
    )
    return (update, residue, search, weights.astype(jnp.bfloat16))


def body(residual, direction, diagonal, recycled, recycled_images, coupling_inverse):
    precise = lax.Precision.HIGHEST
    search_basis = [direction]
    residue_basis = [residual]
    earlier = None
    packed = jnp.stack([direction, residual, diagonal])
    padded = extended(packed, (("gx", 1), ("gy", 2), ("gz", 3)), S)
    wide_diag = padded[2]
    current = padded[:2]
    for iteration in range(S):
        if iteration == S - 1:
            current = current[:1]
            earlier = earlier[:1]
        centre_cells, beside_all = inside(current)
        margin = S - iteration - 1
        local_diag = trim_margin(wide_diag, iteration + 1)
        previous = None if earlier is None else trim_margin(earlier, 2)
        following = chebyshev_next(centre_cells, beside_all, local_diag, previous)
        earlier, current = (current, following)
        search_basis.append(trim_margin(following[0], margin))
        if following.shape[0] > 1:
            residue_basis.append(trim_margin(following[1], margin))
    basis = jnp.stack(search_basis + residue_basis)
    basis_flat = basis.reshape(basis.shape[0], -1)
    gram_block = lax.dot_general(
        basis_flat,
        basis_flat,
        (((1,), (1,)), ((), ())),
        precision=precise,
        preferred_element_type=jnp.float32,
    )
    rounded = basis_flat.astype(jnp.bfloat16)
    images = recycled_images.reshape(recycled_images.shape[0], -1)
    projections = lax.dot_general(
        images, rounded, (((1,), (1,)), ((), ())), preferred_element_type=jnp.float32
    )
    totals = lax.psum(jnp.concatenate([gram_block, projections], 0), ("gx", "gy", "gz"))
    update, residue, search, weights = coordinates(totals, coupling_inverse)
    shape = residual.shape
    solution_delta = jnp.dot(update, basis_flat, precision=precise).reshape(shape)
    new_residual = jnp.dot(residue, basis_flat, precision=precise).reshape(shape)
    correction = jnp.dot(
        weights, recycled.reshape(recycled.shape[0], -1), preferred_element_type=jnp.float32
    )
    new_direction = (jnp.dot(search, basis_flat, precision=precise) - correction).reshape(shape)
    return (solution_delta, new_residual, new_direction)


def solution(mesh):
    in_specs = (
        P("gx", "gy", "gz"),
        P("gx", "gy", "gz"),
        P("gx", "gy", "gz"),
        P(None, "gx", "gy", "gz"),
        P(None, "gx", "gy", "gz"),
        P(),
    )
    out_specs = (P("gx", "gy", "gz"), P("gx", "gy", "gz"), P("gx", "gy", "gz"))
    return jax.shard_map(body, mesh=mesh, in_specs=in_specs, out_specs=out_specs, check_vma=False)
```

profile of v0, /device:TPU:0, one launch (start us, length us, event | category | flops | bytes accessed | tf_op | source)
XLA Modules:
  0.0 110.9 jit_solution(13209403578807758797)
XLA Ops:
  0.7 1.1 %pad_maximum_fusion.2 = f32[3,8,32,128]{3,2,1,0:T(8,128)S(1)} fusion(f32[1,8,32,128]{3,2,1,0:T(8,128)} %bitcast.257, f32[1,8,32,128]{3,2,1,0:T(8,128)} %bitcast.251, f32[1,8,32,128]{3,2,1,0:T(8,128)} %bitcast.245), kind=kLoop, calls=%fused_computation.81 | loop fusion | flops 196608 | bytes 786432 | tf_op jit(solution)/shard_map/stack | solution.py:96
  2.4 2.0 %collective-permute-start.1 = (f32[3,4,32,128]{3,2,1,0:T(8,128)S(1)}, f32[3,4,32,128]{3,2,1,0:T(8,128)S(1)}, u32[]{:S(2)}, u32[]{:S(2)}) collective-permute-start(f32[3,4,32,128]{3,2,1,0:T(8,128)S(1)} %get-tuple-element.14), channel_id=1, source_target_pairs={{8,0},{16,8},{24,16},{0,24},{9,1},{17,9},{25,17},{1,25},{10,2},{18... | collective-permute-start | bytes 589832 | tf_op jit(solution)/shard_map/ppermute | solution.py:24
  4.4 3.3 %collective-permute-done = f32[3,4,32,128]{3,2,1,0:T(8,128)S(1)} collective-permute-done((f32[3,4,32,128]{3,2,1,0:T(8,128)S(1)}, f32[3,4,32,128]{3,2,1,0:T(8,128)S(1)}, u32[]{:S(2)}, u32[]{:S(2)}) %collective-permute-start) | collective-permute-done | bytes 196640 | tf_op jit(solution)/shard_map/ppermute | solution.py:21
  7.7 1.9 %collective-permute-done.1 = f32[3,4,32,128]{3,2,1,0:T(8,128)S(1)} collective-permute-done((f32[3,4,32,128]{3,2,1,0:T(8,128)S(1)}, f32[3,4,32,128]{3,2,1,0:T(8,128)S(1)}, u32[]{:S(2)}, u32[]{:S(2)}) %collective-permute-start.1) | collective-permute-done | bytes 196640 | tf_op jit(solution)/shard_map/ppermute | solution.py:24
  9.6 0.9 pad_maximum_fusion.7
  10.5 1.6 %collective-permute-start.2 = (f32[3,16,4,128]{3,2,1,0:T(4,128)S(1)}, f32[3,16,4,128]{3,2,1,0:T(4,128)S(1)}, u32[]{:S(2)}, u32[]{:S(2)}) collective-permute-start(f32[3,16,4,128]{3,2,1,0:T(4,128)S(1)} %get-tuple-element.11), channel_id=1, source_target_pairs={{0,2},{2,4},{4,6},{6,0},{1,3},{3,5},{5,7},{7,1},{8,10},{10,12},{12... | collective-permute-start | bytes 294920 | tf_op jit(solution)/shard_map/ppermute | solution.py:21
  12.1 2.2 %collective-permute-start.3 = (f32[3,16,4,128]{3,2,1,0:T(4,128)S(1)}, f32[3,16,4,128]{3,2,1,0:T(4,128)S(1)}, u32[]{:S(2)}, u32[]{:S(2)}) collective-permute-start(f32[3,16,4,128]{3,2,1,0:T(4,128)S(1)} %get-tuple-element.12), channel_id=1, source_target_pairs={{2,0},{4,2},{6,4},{0,6},{3,1},{5,3},{7,5},{1,7},{10,8},{12,10},{14... | collective-permute-start | bytes 294920 | tf_op jit(solution)/shard_map/ppermute | solution.py:24
  14.4 3.7 %collective-permute-done.2 = f32[3,16,4,128]{3,2,1,0:T(4,128)S(1)} collective-permute-done((f32[3,16,4,128]{3,2,1,0:T(4,128)S(1)}, f32[3,16,4,128]{3,2,1,0:T(4,128)S(1)}, u32[]{:S(2)}, u32[]{:S(2)}) %collective-permute-start.2) | collective-permute-done | bytes 98336 | tf_op jit(solution)/shard_map/ppermute | solution.py:21
  18.0 1.4 %collective-permute-done.3 = f32[3,16,4,128]{3,2,1,0:T(4,128)S(1)} collective-permute-done((f32[3,16,4,128]{3,2,1,0:T(4,128)S(1)}, f32[3,16,4,128]{3,2,1,0:T(4,128)S(1)}, u32[]{:S(2)}, u32[]{:S(2)}) %collective-permute-start.3) | collective-permute-done | bytes 98336 | tf_op jit(solution)/shard_map/ppermute | solution.py:24
  20.3 1.6 %collective-permute-start.4 = (f32[3,16,40,4]{2,1,3,0:T(8,128)S(1)}, f32[3,16,40,4]{2,1,3,0:T(8,128)S(1)}, u32[]{:S(2)}, u32[]{:S(2)}) collective-permute-start(f32[3,16,40,4]{2,1,3,0:T(8,128)S(1)} %copy.18), channel_id=1, source_target_pairs={{0,1},{1,0},{2,3},{3,2},{4,5},{5,4},{6,7},{7,6},{8,9},{9,8},{10,11... | collective-permute-start | bytes 92168 | tf_op jit(solution)/shard_map/ppermute | solution.py:21
  22.9 2.8 %collective-permute-done.4 = f32[3,16,40,4]{2,1,3,0:T(8,128)S(1)} collective-permute-done((f32[3,16,40,4]{2,1,3,0:T(8,128)S(1)}, f32[3,16,40,4]{2,1,3,0:T(8,128)S(1)}, u32[]{:S(2)}, u32[]{:S(2)}) %collective-permute-start.4) | collective-permute-done | bytes 30752 | tf_op jit(solution)/shard_map/ppermute | solution.py:21
  26.1 1.0 collective-permute-done.5
  27.5 1.1 pad_maximum_fusion
  29.2 1.9 %fusion.6 = f32[2,14,38,134]{3,2,1,0:T(8,128)S(1)} fusion(f32[3,16,40,136]{3,2,1,0:T(8,128)S(1)} %pad_maximum_fusion, f32[14,38,134]{2,1,0:T(8,128)S(1)} %slice_add_fusion.15), kind=kLoop, calls=%fused_computation.8 | loop fusion | flops 1425760 | bytes 4847584 | tf_op jit(solution)/shard_map/div | solution.py:45
  31.1 1.9 %slice_subtract_fusion = f32[2,12,36,132]{3,2,1,0:T(8,128)S(1)} fusion(f32[3,16,40,136]{3,2,1,0:T(8,128)S(1)} %pad_maximum_fusion, f32[2,14,38,134]{3,2,1,0:T(8,128)S(1)} %fusion.6, f32[12,36,132]{2,1,0:T(8,128)S(1)} %slice_add_fusion.16), kind=kLoop, calls=%fused_computation.43 | loop fusion | flops 1254528 | bytes 4333824 | tf_op jit(solution)/shard_map/sub | solution.py:48
  33.0 1.6 %slice_subtract_fusion.1 = f32[2,10,34,130]{3,2,1,0:T(8,128)S(1)} fusion(f32[2,14,38,134]{3,2,1,0:T(8,128)S(1)} %fusion.6, f32[2,12,36,132]{3,2,1,0:T(8,128)S(1)} %slice_subtract_fusion, f32[10,34,130]{2,1,0:T(8,128)S(1)} %slice_add_fusion.17), kind=kLoop, calls=%fused_computation.53 | loop fusion | flops 972400 | bytes 3359200 | tf_op jit(solution)/shard_map/sub | solution.py:48
  35.8 2.1 %stack.65 = f32[9,8,32,128]{3,0,2,1:T(8,128)S(1)} concatenate(f32[1,8,32,128]{3,0,2,1:T(1,128)S(1)} %bitcast.249, f32[1,8,32,128]{3,0,2,1:T(1,128)S(1)} %bitcast.273, f32[1,8,32,128]{3,0,2,1:T(1,128)S(1)} %bitcast.267, f32[1,8,32,128]{3,0,2,1:T(1,128)S(1)} %bitcast.263, f32[1,8,32,128]{3,0,2,1:T(1,128)S(1)} %bitcast.261, f32[1,8,32,128]{3,0,2,1:T(1,128)S(1)} %bitcast.255, ...), dimensions={0} | concatenate | bytes 2359296 | tf_op jit(solution)/shard_map/stack | solution.py:113
  37.8 2.9 %convolution_bitcast_fusion.1 = f32[9,9]{0,1:T(8,128)S(1)} fusion(f32[9,8,32,128]{3,0,2,1:T(8,128)S(1)} %stack.65), kind=kOutput, calls=%fused_computation.14 | convolution fusion | flops 31850496 | bytes 1179972 | tf_op jit(solution)/shard_map/dot_general | solution.py:115
  40.7 1.9 %stack.75 = f32[9,32768]{1,0:T(8,128)S(1)} concatenate(f32[1,32768]{1,0:T(1,128)S(1)} %bitcast.250, f32[1,32768]{1,0:T(1,128)S(1)} %bitcast.274, f32[1,32768]{1,0:T(1,128)S(1)} %bitcast.268, f32[1,32768]{1,0:T(1,128)S(1)} %bitcast.264, f32[1,32768]{1,0:T(1,128)S(1)} %bitcast.262, f32[1,32768]{1,0:T(1,128)S(1)} %bitcast.256, f32[1,32768]{1,0:T(1,128)S(1)} %bitcast.272, ...), dimensions={0} | concatenate | bytes 2359296 | tf_op jit(solution)/shard_map/stack | solution.py:113
  42.6 2.0 %convolution_bitcast_fusion = f32[16,9]{0,1:T(8,128)S(1)} fusion(bf16[2,8,256,128]{3,2,1,0:T(8,128)(2,1)} %bitcast.275, f32[9,32768]{1,0:T(8,128)S(1)} %stack.75), kind=kOutput, calls=%fused_computation.13 | convolution fusion | flops 9732096 | bytes 2228800 | tf_op jit(solution)/shard_map/dot_general | solution.py:124
  44.7 40.0 %psum.7 = f32[25,9]{0,1:T(8,128)S(1)} all-reduce(f32[25,9]{0,1:T(8,128)S(1)} %pad_maximum_fusion.8), channel_id=1, replica_groups=mesh['gx'=4,'gy'=4,'gz'=2] {'gx','gy','gz'}, use_global_device_ids=true, to_apply=%region_0.0 | all-reduce | flops 225 | bytes 1800 | tf_op jit(solution)/shard_map/psum | solution.py:127
  85.4 0.7 fusion.30
  87.5 0.7 fusion.32
  89.7 0.8 fusion.33
  91.8 0.7 fusion.34
  94.0 0.8 fusion.35
  96.1 0.8 fusion.36
  98.5 0.8 fusion.37
  100.8 0.7 fusion.38
  102.1 2.4 %fusion = f32[1,8,32,128]{3,0,2,1:T(1,128)} fusion(f32[8,32,128,9]{2,1,0,3:T(8,128)S(1)} %bitcast.242, f32[9]{0:T(128)S(1)} %fusion.67), kind=kOutput, calls=%fused_computation | convolution fusion | flops 3538944 | bytes 1310756 | tf_op jit(solution)/shard_map/dot_general | solution.py:131
  104.5 2.4 %fusion.2 = f32[1,8,32,128]{3,0,2,1:T(1,128)} fusion(f32[8,32,128,9]{2,1,0,3:T(8,128)S(1)} %bitcast.243, f32[9]{0:T(128)S(1)} %multiply_add_fusion, f32[9]{0:T(128)S(1)} %multiply_add_fusion.1, f32[9]{0:T(128)S(1)} %select_add_fusion, f32[]{:T(128)S(6)} %div.44, f32[]{:T(128)S(6)} %div.42, f32[]{:T(128)S(6)} %div.40, f32[]{:T(128)S(6)} %div.38), kind=kOutput, calls=%fused_computation.2 | convolution fusion | flops 3539016 | bytes 1310844 | tf_op jit(solution)/shard_map/dot_general | solution.py:130
  108.3 1.1 %fusion.62 = f32[1,32768]{1,0:T(1,128)S(1)} fusion(f32[9,32768]{1,0:T(8,128)S(1)} %stack.75, f32[9]{0:T(128)S(1)} %fusion.67, f32[9]{0:T(128)S(1)} %multiply_add_fusion, f32[]{:T(128)S(6)} %div.45), kind=kOutput, calls=%fused_computation.119 | convolution fusion | flops 3538962 | bytes 1310796 | tf_op jit(solution)/shard_map/dot_general | solution.py:135
  (53 shorter events, 8.6 us)
Async XLA Ops:
  0.6 108.8 %copy-start = (f32[16,16]{1,0:T(8,128)S(1)}, f32[16,16]{1,0:T(8,128)}, u32[]{:S(2)}) copy-start(f32[16,16]{1,0:T(8,128)} %param.12) | copy-start | bytes 3076
  0.6 18.8 %copy-start.1 = (f32[8,32,128]{2,1,0:T(8,128)S(1)}, f32[8,32,128]{2,1,0:T(8,128)}, u32[]{:S(2)}) copy-start(f32[8,32,128]{2,1,0:T(8,128)} %param.8) | copy-start | bytes 393220
  0.7 18.8 %copy-start.2 = (f32[8,32,128]{2,1,0:T(8,128)S(1)}, f32[8,32,128]{2,1,0:T(8,128)}, u32[]{:S(2)}) copy-start(f32[8,32,128]{2,1,0:T(8,128)} %param.7) | copy-start | bytes 393220
  0.7 18.8 %copy-start.3 = (f32[8,32,128]{2,1,0:T(8,128)S(1)}, f32[8,32,128]{2,1,0:T(8,128)}, u32[]{:S(2)}) copy-start(f32[8,32,128]{2,1,0:T(8,128)} %param.9) | copy-start | bytes 393220
  1.8 5.8 %collective-permute-start = (f32[3,4,32,128]{3,2,1,0:T(8,128)S(1)}, f32[3,4,32,128]{3,2,1,0:T(8,128)S(1)}, u32[]{:S(2)}, u32[]{:S(2)}) collective-permute-start(f32[3,4,32,128]{3,2,1,0:T(8,128)S(1)} %get-tuple-element.13), channel_id=1, source_target_pairs={{0,8},{8,16},{16,24},{24,0},{1,9},{9,17},{17,25},{25,1},{2,10},{10... | collective-permute-start | bytes 589832 | tf_op jit(solution)/shard_map/ppermute | solution.py:21
  2.4 7.2 %collective-permute-start.1 = (f32[3,4,32,128]{3,2,1,0:T(8,128)S(1)}, f32[3,4,32,128]{3,2,1,0:T(8,128)S(1)}, u32[]{:S(2)}, u32[]{:S(2)}) collective-permute-start(f32[3,4,32,128]{3,2,1,0:T(8,128)S(1)} %get-tuple-element.14), channel_id=1, source_target_pairs={{8,0},{16,8},{24,16},{0,24},{9,1},{17,9},{25,17},{1,25},{10,2},{18... | collective-permute-start | bytes 589832 | tf_op jit(solution)/shard_map/ppermute | solution.py:24
  10.5 7.5 %collective-permute-start.2 = (f32[3,16,4,128]{3,2,1,0:T(4,128)S(1)}, f32[3,16,4,128]{3,2,1,0:T(4,128)S(1)}, u32[]{:S(2)}, u32[]{:S(2)}) collective-permute-start(f32[3,16,4,128]{3,2,1,0:T(4,128)S(1)} %get-tuple-element.11), channel_id=1, source_target_pairs={{0,2},{2,4},{4,6},{6,0},{1,3},{3,5},{5,7},{7,1},{8,10},{10,12},{12... | collective-permute-start | bytes 294920 | tf_op jit(solution)/shard_map/ppermute | solution.py:21
  12.1 7.3 %collective-permute-start.3 = (f32[3,16,4,128]{3,2,1,0:T(4,128)S(1)}, f32[3,16,4,128]{3,2,1,0:T(4,128)S(1)}, u32[]{:S(2)}, u32[]{:S(2)}) collective-permute-start(f32[3,16,4,128]{3,2,1,0:T(4,128)S(1)} %get-tuple-element.12), channel_id=1, source_target_pairs={{2,0},{4,2},{6,4},{0,6},{3,1},{5,3},{7,5},{1,7},{10,8},{12,10},{14... | collective-permute-start | bytes 294920 | tf_op jit(solution)/shard_map/ppermute | solution.py:24
  19.9 2.9 %copy-start.5 = (f32[9,9]{1,0:T(8,128)S(1)}, f32[9,9]{1,0:T(8,128)}, u32[]{:S(2)}) copy-start(f32[9,9]{1,0:T(8,128)} %constant.17.clone) | copy-start | bytes 976
  20.3 5.4 %collective-permute-start.4 = (f32[3,16,40,4]{2,1,3,0:T(8,128)S(1)}, f32[3,16,40,4]{2,1,3,0:T(8,128)S(1)}, u32[]{:S(2)}, u32[]{:S(2)}) collective-permute-start(f32[3,16,40,4]{2,1,3,0:T(8,128)S(1)} %copy.18), channel_id=1, source_target_pairs={{0,1},{1,0},{2,3},{3,2},{4,5},{5,4},{6,7},{7,6},{8,9},{9,8},{10,11... | collective-permute-start | bytes 92168 | tf_op jit(solution)/shard_map/ppermute | solution.py:21
  22.2 4.9 %collective-permute-start.5 = (f32[3,16,40,4]{2,1,3,0:T(8,128)S(1)}, f32[3,16,40,4]{2,1,3,0:T(8,128)S(1)}, u32[]{:S(2)}, u32[]{:S(2)}) collective-permute-start(f32[3,16,40,4]{2,1,3,0:T(8,128)S(1)} %copy.19), channel_id=1, source_target_pairs={{1,0},{0,1},{3,2},{2,3},{5,4},{4,5},{7,6},{6,7},{9,8},{8,9},{11,10... | collective-permute-start | bytes 92168 | tf_op jit(solution)/shard_map/ppermute | solution.py:24
  104.5 5.1 %copy-start.4 = (bf16[16,8,32,128]{3,2,1,0:T(8,128)(2,1)S(1)}, bf16[16,8,32,128]{3,2,1,0:T(8,128)(2,1)}, u32[]{:S(2)}) copy-start(bf16[16,8,32,128]{3,2,1,0:T(8,128)(2,1)} %param.10) | copy-start | bytes 3145732
where the time goes:
time: 111 us
  blocking collectives  40 us (36%)
  matrix products  19.1 us (17%)
  waiting for transfers between devices  14 us (13%)
  between operations  11.8 us (11%)
  other arithmetic  10.2 us (9%)
  starting transfers between devices  8.58 us (8%)
  local copies, waits for them, and re-layouts  7.23 us (7%)
    psum x1, blocking collectives, body(): lax.psum(jnp.concatenate([gram_block, projections], 0), ('gx', 'gy', 'gz'))  40 us
    ppermute x3, waiting for transfers between devices, extended(): lax.ppermute(lax.slice_in_dim(block, block.shape[dim] - width, None, axis...  9.69 us
    ppermute x3, starting transfers between devices, extended(): lax.ppermute(lax.slice_in_dim(block, 0, width, axis=dim), axis, backward)  4.85 us
    ppermute x3, waiting for transfers between devices, extended(): lax.ppermute(lax.slice_in_dim(block, 0, width, axis=dim), axis, backward)  4.3 us
    another operation x2, local copies, waits for them, and re-layouts, body(): basis = jnp.stack(search_basis + residue_basis)  3.93 us
    sub x3, other arithmetic, chebyshev_next(): return 2.0 * scaled - earlier  3.83 us
    dot_general x5, matrix products, coordinates(): jnp.dot(gram_block, residue, precision=precise)  3.78 us
    ppermute x3, starting transfers between devices, extended(): lax.ppermute(lax.slice_in_dim(block, block.shape[dim] - width, None, axis...  3.73 us
  transfers between devices with their start and end apart: 6, of which 6 were waited for; matrix products, arithmetic and copies ran while one was open for 1% of the time, Pallas kernels for 0%

commit v1 on v0

--- a/solution.py
+++ b/solution.py
@@ -1,11 +1,17 @@
 import jax
 import jax.numpy as jnp
-import numpy as np
 from jax import lax
+from jax.experimental import pallas as pl
+from jax.experimental.pallas import tpu as pltpu
 from jax.sharding import PartitionSpec as P
 
 S = 4
 BASIS = 9
+RECYCLED = 16
+LANES = 128
+PROJECTED = 16
+SECOND = 32
+AXES = ("gx", "gy", "gz")
 
 
 center = 7.25
@@ -48,44 +54,71 @@
     return 2.0 * scaled - earlier
 
 
-def recurrence_matrix():
-    recurrence = np.zeros((BASIS, BASIS), np.float32)
-    for offset, length in ((0, S + 1), (S + 1, S)):
-        recurrence[offset, offset] = center
-        recurrence[offset + 1, offset] = half_width
-        for column in range(1, length - 1):
-            recurrence[offset + column + 1, offset + column] = half_width / 2
-            recurrence[offset + column, offset + column] = center
-            recurrence[offset + column - 1, offset + column] = half_width / 2
-    return jnp.asarray(recurrence, dtype=jnp.float32)
+def finish_kernel(parts, coupling, basis, recycled, delta_out, residual_out, direction_out):
+    rows = 16
+    total = jnp.sum(parts[...], axis=0)
+    lane = lax.broadcasted_iota(jnp.int32, (rows, LANES), 1)
+    row = lax.broadcasted_iota(jnp.int32, (rows, LANES), 0)
+    table = jnp.concatenate([total, pltpu.roll(total, LANES - SECOND, 1)], axis=0)
+    gram = jnp.where(lane < BASIS, table, 0.0)
+    images = jnp.where(lane < RECYCLED, pltpu.roll(table, LANES - PROJECTED, 1), 0.0)
 
+    def bands(index):
+        first = (index == 0) | (index == S + 1)
+        last = (index == S) | (index >= BASIS - 1)
+        before_last = (index == S - 1) | (index == BASIS - 2)
+        second = (index == 1) | (index == S + 2)
+        middle = jnp.where(last, 0.0, center)
+        below = jnp.where(first | (index >= BASIS), 0.0, jnp.where(second, half_width, half_width / 2))
+        above = jnp.where(last | before_last, 0.0, half_width / 2)
+        return (middle, below, above)
 
-def coordinates(totals, coupling_inverse):
-    precise = lax.Precision.HIGHEST
-    gram_block = totals[:BASIS]
-    projections = totals[BASIS:]
-    recurrence = recurrence_matrix()
-    counter = jnp.arange(BASIS)
-    residue = (counter == S + 1).astype(jnp.float32)
-    search = (counter == 0).astype(jnp.float32)
-    update = jnp.zeros((BASIS,), jnp.float32)
-    norm_now = jnp.dot(residue, jnp.dot(gram_block, residue, precision=precise), precision=precise)
+    by_row = bands(row)
+    by_lane = bands(lane)
+
+    def apply(coefficients, values, axis, size):
+        middle, below, above = coefficients
+        return (
+            middle * values
+            + below * pltpu.roll(values, 1, axis)
+            + above * pltpu.roll(values, size - 1, axis)
+        )
+
+    def form(down, across):
+        product = gram * down * across
+        return jnp.sum(jnp.sum(product, axis=0, keepdims=True), axis=1, keepdims=True)
+
+    residue = [(row == S + 1).astype(jnp.float32), (lane == S + 1).astype(jnp.float32)]
+    search = [(row == 0).astype(jnp.float32), (lane == 0).astype(jnp.float32)]
+    update = jnp.zeros((rows, LANES), jnp.float32)
+    norm_now = form(residue[0], residue[1])
     for iteration in range(S):
-        mapped = jnp.dot(recurrence, search, precision=precise)
-        step_size = norm_now / jnp.dot(
-            search, jnp.dot(gram_block, mapped, precision=precise), precision=precise
-        )
-        update = update + step_size * search
-        residue = residue - step_size * mapped
-        norm_next = jnp.dot(
-            residue, jnp.dot(gram_block, residue, precision=precise), precision=precise
-        )
-        search = residue + norm_next / norm_now * search
+        mapped = [apply(by_row, search[0], 0, rows), apply(by_lane, search[1], 1, LANES)]
+        step_size = norm_now / form(search[0], mapped[1])
+        update = update + step_size * search[0]
+        residue = [residue[0] - step_size * mapped[0], residue[1] - step_size * mapped[1]]
+        norm_next = form(residue[0], residue[1])
+        ratio = norm_next / norm_now
+        search = [residue[0] + ratio * search[0], residue[1] + ratio * search[1]]
         norm_now = norm_next
-    weights = jnp.dot(
-        coupling_inverse, jnp.dot(projections, residue, precision=precise), precision=precise
-    )
-    return (update, residue, search, weights.astype(jnp.bfloat16))
+    projected = jnp.sum(images * residue[0], axis=0, keepdims=True)[:, :RECYCLED]
+    weights = jnp.sum(coupling[...] * projected, axis=1, keepdims=True)
+    weights = jnp.broadcast_to(weights.astype(jnp.bfloat16).astype(jnp.float32), (RECYCLED, LANES))
+    for plane in range(delta_out.shape[0]):
+        delta = 0.0
+        left = 0.0
+        ahead = 0.0
+        for field in range(BASIS):
+            values = basis[field, plane]
+            delta = delta + update[field : field + 1] * values
+            left = left + residue[0][field : field + 1] * values
+            ahead = ahead + search[0][field : field + 1] * values
+        correction = 0.0
+        for vector in range(RECYCLED):
+            correction = correction + weights[vector : vector + 1] * recycled[vector, plane].astype(jnp.float32)
+        delta_out[plane] = delta
+        residual_out[plane] = left
+        direction_out[plane] = ahead - correction
 
 
 def body(residual, direction, diagonal, recycled, recycled_images, coupling_inverse):
@@ -124,16 +157,21 @@
     projections = lax.dot_general(
         images, rounded, (((1,), (1,)), ((), ())), preferred_element_type=jnp.float32
     )
-    totals = lax.psum(jnp.concatenate([gram_block, projections], 0), ("gx", "gy", "gz"))
-    update, residue, search, weights = coordinates(totals, coupling_inverse)
-    shape = residual.shape
-    solution_delta = jnp.dot(update, basis_flat, precision=precise).reshape(shape)
-    new_residual = jnp.dot(residue, basis_flat, precision=precise).reshape(shape)
-    correction = jnp.dot(
-        weights, recycled.reshape(recycled.shape[0], -1), preferred_element_type=jnp.float32
-    )
-    new_direction = (jnp.dot(search, basis_flat, precision=precise) - correction).reshape(shape)
-    return (solution_delta, new_residual, new_direction)
+    table = jnp.zeros((BASIS, LANES), jnp.float32)
+    table = table.at[:, :BASIS].set(gram_block).at[:, PROJECTED : PROJECTED + RECYCLED].set(projections.T)
+    last = jnp.roll(table[BASIS - 1 :], SECOND, 1)
+    table = table[: BASIS - 1] + jnp.pad(last, ((0, BASIS - 2), (0, 0)))
+    devices = lax.axis_size(AXES)
+    parts = lax.all_to_all(jnp.broadcast_to(table[None], (devices, BASIS - 1, LANES)), AXES, 0, 0)
+    field = jax.ShapeDtypeStruct(residual.shape, jnp.float32)
+    in_vmem = pl.BlockSpec(memory_space=pltpu.VMEM)
+    return pl.pallas_call(
+        finish_kernel,
+        out_shape=(field, field, field),
+        in_specs=[in_vmem] * 4,
+        out_specs=(in_vmem, in_vmem, in_vmem),
+        name="finish",
+    )(parts, coupling_inverse, basis, recycled)
 
 
 def solution(mesh):

time: 111 us -> 68.5 us (0.62)
  blocking collectives: 40 us -> 11.8 us
  matrix products: 19.1 us -> 6.47 us
  between operations: 11.8 us -> 0.98 us
  local copies, waits for them, and re-layouts: 7.23 us -> 12.9 us
  Pallas kernels: 0 us -> 3.72 us
  waiting for transfers between devices: 14 us -> 11.6 us
  other arithmetic: 10.2 us -> 12 us
    psum x1 -> x0, blocking collectives: 40 us -> none  [body(): lax.psum(jnp.concatenate([gram_block, projections], 0), ('gx', 'gy', 'gz'))]
    dot_general x19 -> x0, matrix products: 14.2 us -> none  [the longest x5 3.78 us: coordinates(): jnp.dot(gram_block, residue, precision=precise)]
    all_to_all x0 -> x1, blocking collectives: none -> 11.8 us  [body(): lax.all_to_all(jnp.broadcast_to(table[None], (devices, BASIS - 1, LANES))...]
    pallas_call x0 -> x1, Pallas kernels: none -> 3.72 us  [body(): pl.pallas_call(finish_kernel, out_shape=(field, field, field), in_specs=[...]
    another operation x2 -> x10, local copies, waits for them, and re-layouts: 3.93 us -> 7.09 us  [body(): basis = jnp.stack(search_basis + residue_basis)]
    ppermute x3, waiting for transfers between devices: 9.69 us -> 7.21 us  [extended(): lax.ppermute(lax.slice_in_dim(block, block.shape[dim] - width, None, axis...]
    concatenate x2, other arithmetic: 1.19 us -> 3.25 us  [extended(): block = jnp.concatenate([low, block, high], axis=dim)]
    another operation x0 -> x5, other arithmetic: none -> 1.67 us
  transfers between devices with their start and end apart: 6 -> 6, of which waited for: 6 -> 6; matrix products, arithmetic and copies ran while one was open for 1% -> 5% of each run, Pallas kernels for 0% -> 0%
where the time goes in v1:
time: 68.5 us; the launch traced here: 68.1 us
  local copies, waits for them, and re-layouts  12.9 us (19%)
  other arithmetic  12 us (18%)
  blocking collectives  11.8 us (17%)
  waiting for transfers between devices  11.6 us (17%)
  starting transfers between devices  8.58 us (13%)
  matrix products  6.47 us (9%)
  Pallas kernels  3.72 us (5%)
  between operations  0.98 us (1%)
    all_to_all x1, blocking collectives, body(): lax.all_to_all(jnp.broadcast_to(table[None], (devices, BASIS - 1, LANES))...  11.8 us
    ppermute x3, waiting for transfers between devices, extended(): lax.ppermute(lax.slice_in_dim(block, block.shape[dim] - width, None, axis...  7.21 us
    another operation x10, local copies, waits for them, and re-layouts, body(): basis = jnp.stack(search_basis + residue_basis)  7.09 us
    ppermute x3, starting transfers between devices, extended(): lax.ppermute(lax.slice_in_dim(block, 0, width, axis=dim), axis, backward)  4.85 us
    ppermute x3, waiting for transfers between devices, extended(): lax.ppermute(lax.slice_in_dim(block, 0, width, axis=dim), axis, backward)  4.42 us
    dot_general x1, matrix products, body(): lax.dot_general(basis_flat, basis_flat, (((1,), (1,)), ((), ())), precisi...  3.91 us
    ppermute x3, starting transfers between devices, extended(): lax.ppermute(lax.slice_in_dim(block, block.shape[dim] - width, None, axis...  3.73 us
    pallas_call x1, Pallas kernels, body(): pl.pallas_call(finish_kernel, out_shape=(field, field, field), in_specs=[...  3.72 us
  transfers between devices with their start and end apart: 6, of which 6 were waited for; matrix products, arithmetic and copies ran while one was open for 5% of the time, Pallas kernels for 0%

profile of v1, /device:TPU:0, one launch (start us, length us, event | category | flops | bytes accessed | tf_op | source)
XLA Modules:
  0.0 68.1 jit_solution(16855863728891386181)
XLA Ops:
  0.7 1.1 %pad_maximum_fusion.2 = f32[3,8,32,128]{3,2,1,0:T(8,128)S(1)} fusion(f32[1,8,32,128]{3,2,1,0:T(8,128)} %bitcast.63, f32[1,8,32,128]{3,2,1,0:T(8,128)} %bitcast.59, f32[1,8,32,128]{3,2,1,0:T(8,128)} %bitcast.55), kind=kLoop, calls=%fused_computation.45 | loop fusion | flops 196608 | bytes 786432 | tf_op jit(solution)/shard_map/stack | solution.py:129
  2.4 2.0 %collective-permute-start.1 = (f32[3,4,32,128]{3,2,1,0:T(8,128)S(1)}, f32[3,4,32,128]{3,2,1,0:T(8,128)S(1)}, u32[]{:S(2)}, u32[]{:S(2)}) collective-permute-start(f32[3,4,32,128]{3,2,1,0:T(8,128)S(1)} %get-tuple-element.40), channel_id=1, source_target_pairs={{8,0},{16,8},{24,16},{0,24},{9,1},{17,9},{25,17},{1,25},{10,2},{18... | collective-permute-start | bytes 589832 | tf_op jit(solution)/shard_map/ppermute | solution.py:30
  4.4 3.3 %collective-permute-done = f32[3,4,32,128]{3,2,1,0:T(8,128)S(1)} collective-permute-done((f32[3,4,32,128]{3,2,1,0:T(8,128)S(1)}, f32[3,4,32,128]{3,2,1,0:T(8,128)S(1)}, u32[]{:S(2)}, u32[]{:S(2)}) %collective-permute-start) | collective-permute-done | bytes 196640 | tf_op jit(solution)/shard_map/ppermute | solution.py:27
  7.6 1.9 %collective-permute-done.1 = f32[3,4,32,128]{3,2,1,0:T(8,128)S(1)} collective-permute-done((f32[3,4,32,128]{3,2,1,0:T(8,128)S(1)}, f32[3,4,32,128]{3,2,1,0:T(8,128)S(1)}, u32[]{:S(2)}, u32[]{:S(2)}) %collective-permute-start.1) | collective-permute-done | bytes 196640 | tf_op jit(solution)/shard_map/ppermute | solution.py:30
  9.6 1.6 %collective-permute-start.2 = (f32[3,16,4,128]{3,2,1,0:T(4,128)S(1)}, f32[3,16,4,128]{3,2,1,0:T(4,128)}, u32[]{:S(2)}, u32[]{:S(2)}) collective-permute-start(f32[3,16,4,128]{3,2,1,0:T(4,128)S(1)} %get-tuple-element.37), channel_id=1, source_target_pairs={{0,2},{2,4},{4,6},{6,0},{1,3},{3,5},{5,7},{7,1},{8,10},{10,12},{12... | collective-permute-start | bytes 294920 | tf_op jit(solution)/shard_map/ppermute | solution.py:27
  11.3 2.2 %collective-permute-start.3 = (f32[3,16,4,128]{3,2,1,0:T(4,128)S(1)}, f32[3,16,4,128]{3,2,1,0:T(4,128)}, u32[]{:S(2)}, u32[]{:S(2)}) collective-permute-start(f32[3,16,4,128]{3,2,1,0:T(4,128)S(1)} %get-tuple-element.38), channel_id=1, source_target_pairs={{2,0},{4,2},{6,4},{0,6},{3,1},{5,3},{7,5},{1,7},{10,8},{12,10},{14... | collective-permute-start | bytes 294920 | tf_op jit(solution)/shard_map/ppermute | solution.py:30
  13.5 3.8 %collective-permute-done.2 = f32[3,16,4,128]{3,2,1,0:T(4,128)} collective-permute-done((f32[3,16,4,128]{3,2,1,0:T(4,128)S(1)}, f32[3,16,4,128]{3,2,1,0:T(4,128)}, u32[]{:S(2)}, u32[]{:S(2)}) %collective-permute-start.2) | collective-permute-done | bytes 98336 | tf_op jit(solution)/shard_map/ppermute | solution.py:27
  17.3 1.4 %collective-permute-done.3 = f32[3,16,4,128]{3,2,1,0:T(4,128)} collective-permute-done((f32[3,16,4,128]{3,2,1,0:T(4,128)S(1)}, f32[3,16,4,128]{3,2,1,0:T(4,128)}, u32[]{:S(2)}, u32[]{:S(2)}) %collective-permute-start.3) | collective-permute-done | bytes 98336 | tf_op jit(solution)/shard_map/ppermute | solution.py:30
  18.7 1.1 %pad_maximum_fusion.1 = f32[3,16,40,128]{3,2,1,0:T(8,128)S(1)} fusion(f32[3,16,4,128]{3,2,1,0:T(4,128)} %collective-permute-done.3, f32[3,4,32,128]{3,2,1,0:T(8,128)S(1)} %collective-permute-done.1, f32[1,8,32,128]{3,2,1,0:T(8,128)S(1)} %bitcast.65, f32[1,8,32,128]{3,2,1,0:T(8,128)S(1)} %bitcast.61, f32[1,8,32,128]{3,2,1,0:T(8,128)S(1)} %bitcast.57, ...), kind=kLoop, calls=%fused_computation.25 | loop fusion | flops 1474560 | bytes 1966080 | tf_op jit(solution)/shard_map/concatenate | solution.py:31
  20.5 1.6 %collective-permute-start.4 = (f32[3,16,40,4]{2,1,3,0:T(8,128)S(1)}, f32[3,16,40,4]{2,1,3,0:T(8,128)S(1)}, u32[]{:S(2)}, u32[]{:S(2)}) collective-permute-start(f32[3,16,40,4]{2,1,3,0:T(8,128)S(1)} %copy.11), channel_id=1, source_target_pairs={{0,1},{1,0},{2,3},{3,2},{4,5},{5,4},{6,7},{7,6},{8,9},{9,8},{10,11... | collective-permute-start | bytes 92168 | tf_op jit(solution)/shard_map/ppermute | solution.py:27
  22.4 0.6 collective-permute-start.5
  23.1 0.7 %stack.66 = bf16[1,32768]{1,0:T(2,128)(2,1)} reshape(bf16[8,32,128]{2,1,0:T(8,128)(2,1)S(1)} %convert.36) | data formatting | bytes 131072 | tf_op jit(solution)/shard_map/stack | solution.py:146
  23.7 0.7 %stack.71 = bf16[1,32768]{1,0:T(2,128)(2,1)} reshape(bf16[8,32,128]{2,1,0:T(8,128)(2,1)S(1)} %convert.41) | data formatting | bytes 131072 | tf_op jit(solution)/shard_map/stack | solution.py:146
  24.4 0.7 compare_reduce_fusion.1
  25.1 0.6 compare_reduce_fusion
  26.3 1.1 %collective-permute-done.5 = f32[3,16,40,4]{2,1,3,0:T(8,128)} collective-permute-done((f32[3,16,40,4]{2,1,3,0:T(8,128)S(1)}, f32[3,16,40,4]{2,1,3,0:T(8,128)}, u32[]{:S(2)}, u32[]{:S(2)}) %collective-permute-start.5) | collective-permute-done | bytes 30752 | tf_op jit(solution)/shard_map/ppermute | solution.py:30
  27.4 1.3 %copy.14 = f32[3,16,40,4]{3,2,1,0:T(8,128)S(1)} copy(f32[3,16,40,4]{2,1,3,0:T(8,128)} %collective-permute-done.5) | data formatting | bytes 61440 | tf_op jit(solution)/shard_map/ppermute | solution.py:30
  28.7 2.2 %pad_maximum_fusion = f32[3,16,40,136]{3,2,1,0:T(8,128)S(1)} fusion(f32[3,16,40,4]{3,2,1,0:T(8,128)S(1)} %copy.14, f32[3,16,4,128]{3,2,1,0:T(4,128)} %collective-permute-done.3, f32[3,4,32,128]{3,2,1,0:T(8,128)} %copy-done.5, f32[1,8,32,128]{3,2,1,0:T(8,128)S(1)} %bitcast.66, f32[1,8,32,128]{3,2,1,0:T(8,128)S(1)} %bitcast.62, ...), kind=kLoop, calls=%fused_computation.2 | loop fusion | flops 2088960 | bytes 2088960 | tf_op jit(solution)/shard_map/concatenate | solution.py:31
  31.5 1.9 %fusion.4 = f32[2,14,38,134]{3,2,1,0:T(8,128)S(1)} fusion(f32[3,16,40,136]{3,2,1,0:T(8,128)S(1)} %pad_maximum_fusion, f32[14,38,134]{2,1,0:T(8,128)S(1)} %slice_add_fusion.15), kind=kLoop, calls=%fused_computation.6 | loop fusion | flops 1425760 | bytes 4847584 | tf_op jit(solution)/shard_map/div | solution.py:51
  33.7 1.9 %slice_subtract_fusion = f32[2,12,36,132]{3,2,1,0:T(8,128)S(1)} fusion(f32[3,16,40,136]{3,2,1,0:T(8,128)S(1)} %pad_maximum_fusion, f32[2,14,38,134]{3,2,1,0:T(8,128)S(1)} %fusion.4, f32[12,36,132]{2,1,0:T(8,128)S(1)} %slice_add_fusion.16), kind=kLoop, calls=%fused_computation.16 | loop fusion | flops 1254528 | bytes 4333824 | tf_op jit(solution)/shard_map/sub | solution.py:54
  35.6 0.7 %slice.467 = bf16[8,32,128]{2,1,0:T(8,128)(2,1)} slice(f32[12,36,132]{2,1,0:T(8,128)S(1)} %get-tuple-element.32), slice={[2:10], [2:34], [2:130]} | slice | bytes 131072 | tf_op jit(solution)/shard_map/slice | solution.py:46
  36.4 1.6 %slice_subtract_fusion.1 = f32[2,10,34,130]{3,2,1,0:T(8,128)S(1)} fusion(f32[2,14,38,134]{3,2,1,0:T(8,128)S(1)} %fusion.4, f32[2,12,36,132]{3,2,1,0:T(8,128)S(1)} %slice_subtract_fusion, f32[10,34,130]{2,1,0:T(8,128)S(1)} %slice_add_fusion.17), kind=kLoop, calls=%fused_computation.26 | loop fusion | flops 972400 | bytes 3359200 | tf_op jit(solution)/shard_map/sub | solution.py:54
  38.8 0.9 %stack.68 = bf16[1,32768]{1,0:T(2,128)(2,1)S(1)} reshape(bf16[8,32,128]{2,1,0:T(8,128)(2,1)} %slice.467) | data formatting | bytes 131072 | tf_op jit(solution)/shard_map/stack | solution.py:146
  39.7 0.7 %slice.464 = bf16[8,32,128]{2,1,0:T(8,128)(2,1)} slice(f32[12,36,132]{2,1,0:T(8,128)S(1)} %get-tuple-element.31), slice={[2:10], [2:34], [2:130]} | slice | bytes 131072 | tf_op jit(solution)/shard_map/slice | solution.py:46
  40.4 1.5 %stack.73 = bf16[1,32768]{1,0:T(2,128)(2,1)} reshape(bf16[8,32,128]{2,1,0:T(8,128)(2,1)} %slice.464) | data formatting | bytes 131072 | tf_op jit(solution)/shard_map/stack | solution.py:146
  41.9 0.7 %stack.67 = bf16[1,32768]{1,0:T(2,128)(2,1)} reshape(bf16[8,32,128]{2,1,0:T(8,128)(2,1)S(1)} %slice.468) | data formatting | bytes 131072 | tf_op jit(solution)/shard_map/stack | solution.py:146
  42.7 0.7 stack.72
  43.8 3.9 %fusion.8 = f32[9,9]{1,0:T(8,128)S(1)} fusion(f32[9,8,32,128]{3,2,1,0:T(8,128)S(1)} %bitcast_dynamic-update-slice_fusion.basis, pred[]{:T(512)} %compare_reduce_fusion.1), kind=kOutput, calls=%fused_computation.13 | convolution fusion | flops 31850576 | bytes 1179973 | tf_op jit(solution)/shard_map/dot_general | solution.py:148
  47.8 1.8 %stack.75 = bf16[9,32768]{1,0:T(8,128)(2,1)S(1)} concatenate(bf16[1,32768]{1,0:T(2,128)(2,1)S(1)} %copy-done.6, bf16[1,32768]{1,0:T(2,128)(2,1)S(1)} %copy-done.9, bf16[1,32768]{1,0:T(2,128)(2,1)S(1)} %stack.68, bf16[1,32768]{1,0:T(2,128)(2,1)S(1)} %stack.69, bf16[1,32768]{1,0:T(2,128)(2,1)S(1)} %bitcast.67, bf16[1,32768]{1,0:T(2,128)(2,1)S(1)} %copy-done.7, ...), dimensions={0} | concatenate | bytes 1179648 | tf_op jit(solution)/shard_map/stack | solution.py:146
  49.6 2.6 %convolution_select_fusion = f32[9,16]{1,0:T(8,128)S(1)} fusion(bf16[9,32768]{1,0:T(8,128)(2,1)S(1)} %stack.75, bf16[2,8,256,128]{3,2,1,0:T(8,128)(2,1)} %bitcast.69, pred[]{:T(512)} %compare_reduce_fusion), kind=kOutput, calls=%fused_computation.12 | convolution fusion | flops 9437328 | bytes 1638977 | tf_op jit(solution)/shard_map/dot_general | solution.py:157
  52.6 11.8 %all_to_all.5.parts = f32[32,8,128]{2,1,0:T(8,128)} all-to-all(f32[32,8,128]{2,1,0:T(8,128)S(1)} %broadcast_in_dim.5), channel_id=1, replica_groups=mesh['gx'=4,'gy'=4,'gz'=2] {'gx','gy','gz'}, dimensions={0} | all-to-all | bytes 262144 | tf_op jit(solution)/shard_map/all_to_all | solution.py:165
  64.4 3.7 %finish.1 = (f32[8,32,128]{2,1,0:T(8,128)}, f32[8,32,128]{2,1,0:T(8,128)}, f32[8,32,128]{2,1,0:T(8,128)}) custom-call(f32[32,8,128]{2,1,0:T(8,128)} %all_to_all.5.parts, f32[16,16]{1,0:T(8,128)} %coupling.1, f32[9,8,32,128]{3,2,1,0:T(8,128)} %copy-done, bf16[16,8,32,128]{3,2,1,0:T(8,128)(2,1)} %recycled.1), custom_call_target="tpu_custom_call" | custom-call | tf_op jit(solution)/shard_map/finish/pallas_call | solution.py:168
  (61 shorter events, 5.1 us)
Async XLA Ops:
  0.6 8.9 %copy-start.1 = (f32[8,32,128]{2,1,0:T(8,128)S(1)}, f32[8,32,128]{2,1,0:T(8,128)}, u32[]{:S(2)}) copy-start(f32[8,32,128]{2,1,0:T(8,128)} %param.11) | copy-start | bytes 393220
  0.6 8.9 %copy-start.2 = (f32[8,32,128]{2,1,0:T(8,128)S(1)}, f32[8,32,128]{2,1,0:T(8,128)}, u32[]{:S(2)}) copy-start(f32[8,32,128]{2,1,0:T(8,128)} %param.10) | copy-start | bytes 393220
  0.7 8.9 %copy-start.3 = (f32[8,32,128]{2,1,0:T(8,128)S(1)}, f32[8,32,128]{2,1,0:T(8,128)}, u32[]{:S(2)}) copy-start(f32[8,32,128]{2,1,0:T(8,128)} %param.12) | copy-start | bytes 393220
  1.8 5.8 %collective-permute-start = (f32[3,4,32,128]{3,2,1,0:T(8,128)S(1)}, f32[3,4,32,128]{3,2,1,0:T(8,128)S(1)}, u32[]{:S(2)}, u32[]{:S(2)}) collective-permute-start(f32[3,4,32,128]{3,2,1,0:T(8,128)S(1)} %get-tuple-element.39), channel_id=1, source_target_pairs={{0,8},{8,16},{16,24},{24,0},{1,9},{9,17},{17,25},{25,1},{2,10},{10... | collective-permute-start | bytes 589832 | tf_op jit(solution)/shard_map/ppermute | solution.py:27
  2.4 7.2 %collective-permute-start.1 = (f32[3,4,32,128]{3,2,1,0:T(8,128)S(1)}, f32[3,4,32,128]{3,2,1,0:T(8,128)S(1)}, u32[]{:S(2)}, u32[]{:S(2)}) collective-permute-start(f32[3,4,32,128]{3,2,1,0:T(8,128)S(1)} %get-tuple-element.40), channel_id=1, source_target_pairs={{8,0},{16,8},{24,16},{0,24},{9,1},{17,9},{25,17},{1,25},{10,2},{18... | collective-permute-start | bytes 589832 | tf_op jit(solution)/shard_map/ppermute | solution.py:30
  7.6 11.0 %copy-start.4 = (f32[3,4,32,128]{3,2,1,0:T(8,128)}, f32[3,4,32,128]{3,2,1,0:T(8,128)S(1)}, u32[]{:S(2)}) copy-start(f32[3,4,32,128]{3,2,1,0:T(8,128)S(1)} %collective-permute-done) | copy-start | bytes 589828
  9.6 9.1 %copy-start.5 = (f32[3,4,32,128]{3,2,1,0:T(8,128)}, f32[3,4,32,128]{3,2,1,0:T(8,128)S(1)}, u32[]{:S(2)}) copy-start(f32[3,4,32,128]{3,2,1,0:T(8,128)S(1)} %collective-permute-done.1) | copy-start | bytes 589828
  9.6 7.6 %collective-permute-start.2 = (f32[3,16,4,128]{3,2,1,0:T(4,128)S(1)}, f32[3,16,4,128]{3,2,1,0:T(4,128)}, u32[]{:S(2)}, u32[]{:S(2)}) collective-permute-start(f32[3,16,4,128]{3,2,1,0:T(4,128)S(1)} %get-tuple-element.37), channel_id=1, source_target_pairs={{0,2},{2,4},{4,6},{6,0},{1,3},{3,5},{5,7},{7,1},{8,10},{10,12},{12... | collective-permute-start | bytes 294920 | tf_op jit(solution)/shard_map/ppermute | solution.py:27
  11.3 7.4 %collective-permute-start.3 = (f32[3,16,4,128]{3,2,1,0:T(4,128)S(1)}, f32[3,16,4,128]{3,2,1,0:T(4,128)}, u32[]{:S(2)}, u32[]{:S(2)}) collective-permute-start(f32[3,16,4,128]{3,2,1,0:T(4,128)S(1)} %get-tuple-element.38), channel_id=1, source_target_pairs={{2,0},{4,2},{6,4},{0,6},{3,1},{5,3},{7,5},{1,7},{10,8},{12,10},{14... | collective-permute-start | bytes 294920 | tf_op jit(solution)/shard_map/ppermute | solution.py:30
  20.5 5.4 %collective-permute-start.4 = (f32[3,16,40,4]{2,1,3,0:T(8,128)S(1)}, f32[3,16,40,4]{2,1,3,0:T(8,128)S(1)}, u32[]{:S(2)}, u32[]{:S(2)}) collective-permute-start(f32[3,16,40,4]{2,1,3,0:T(8,128)S(1)} %copy.11), channel_id=1, source_target_pairs={{0,1},{1,0},{2,3},{3,2},{4,5},{5,4},{6,7},{7,6},{8,9},{9,8},{10,11... | collective-permute-start | bytes 92168 | tf_op jit(solution)/shard_map/ppermute | solution.py:27
  22.4 5.0 %collective-permute-start.5 = (f32[3,16,40,4]{2,1,3,0:T(8,128)S(1)}, f32[3,16,40,4]{2,1,3,0:T(8,128)}, u32[]{:S(2)}, u32[]{:S(2)}) collective-permute-start(f32[3,16,40,4]{2,1,3,0:T(8,128)S(1)} %copy.12), channel_id=1, source_target_pairs={{1,0},{0,1},{3,2},{2,3},{5,4},{4,5},{7,6},{6,7},{9,8},{8,9},{11,10... | collective-permute-start | bytes 92168 | tf_op jit(solution)/shard_map/ppermute | solution.py:30
  43.6 4.1 %copy-start.6 = (bf16[1,32768]{1,0:T(2,128)(2,1)S(1)}, bf16[1,32768]{1,0:T(2,128)(2,1)}, u32[]{:S(2)}) copy-start(bf16[1,32768]{1,0:T(2,128)(2,1)} %stack.66) | copy-start | bytes 196612
  43.6 4.1 %copy-start.7 = (bf16[1,32768]{1,0:T(2,128)(2,1)S(1)}, bf16[1,32768]{1,0:T(2,128)(2,1)}, u32[]{:S(2)}) copy-start(bf16[1,32768]{1,0:T(2,128)(2,1)} %stack.71) | copy-start | bytes 196612
  43.7 5.9 %copy-start = (f32[9,8,32,128]{3,2,1,0:T(8,128)}, f32[9,8,32,128]{3,2,1,0:T(8,128)S(1)}, u32[]{:S(2)}) copy-start(f32[9,8,32,128]{3,2,1,0:T(8,128)S(1)} %bitcast_dynamic-update-slice_fusion.basis) | copy-start | bytes 3538948
  43.7 4.0 %copy-start.8 = (bf16[1,32768]{1,0:T(2,128)(2,1)S(1)}, bf16[1,32768]{1,0:T(2,128)(2,1)}, u32[]{:S(2)}) copy-start(bf16[1,32768]{1,0:T(2,128)(2,1)} %stack.73) | copy-start | bytes 196612
  43.8 4.0 %copy-start.9 = (bf16[1,32768]{1,0:T(2,128)(2,1)S(1)}, bf16[1,32768]{1,0:T(2,128)(2,1)}, u32[]{:S(2)}) copy-start(bf16[1,32768]{1,0:T(2,128)(2,1)} %stack.67) | copy-start | bytes 196612
  43.8 4.0 %copy-start.10 = (bf16[1,32768]{1,0:T(2,128)(2,1)S(1)}, bf16[1,32768]{1,0:T(2,128)(2,1)}, u32[]{:S(2)}) copy-start(bf16[1,32768]{1,0:T(2,128)(2,1)} %stack.72) | copy-start | bytes 196612
